TPU v7x, 32 devices: a whole 2x2x4 slice. The times are simulated.
32 devices in a mesh: dom: 32 (over z, y, x, core).
Axes of the slice: x: 2, y: 2, z: 4, core: 2. Of those that a mesh axis runs over, the one named last changes fastest.
Arguments:
- right_side: float32 [1024, 16, 128], P('dom')
- band_blocks: float32 [1024, 5, 128, 128], P('dom'), as said below
- link_blocks: float32 [32, 6, 4, 128, 128], P('dom'), as said below
- link_rows: int32 [32, 6, 4], P('dom'), may hold values from 0 to 32, as said below
Outputs:
- solution: float32 [1024, 16, 128], P('dom')
- residual: float32 [1024, 16, 128], P('dom')
Inputs may be any that keep to these rules, and one draw needn't show every extreme that they name: `link_rows`: entries are a row of device d (0 to 31) or 32 for an unused slot. Slot s of interface j of device d is paired with slot s of interface j xor 1 of the device it faces, and is used exactly when that one is. Each interface uses its first 1 to 4 slots and no row twice; in every draw some interface uses all 4. link_blocks[d, j, s] is the transpose of link_blocks[e, j xor 1, s] for the device e that interface j of d faces; blocks of unused slots are zero. band_blocks[g, 2 + m] is the transpose of band_blocks[g + m, 2 - m]; blocks whose column falls outside the device are zero. A is symmetric with a positive diagonal that exceeds the sum of magnitudes of the rest of its row.
All inputs are finite; a program needn't handle non-finite values.
Results may differ from a plain program's by a relative error of at most 0.0003.
Values sent between devices are 32-bit elements; how exact they have to be, the bound alone decides.
A program may use at most 64 MiB of HBM per device.

v0:
```python
import functools

import jax
import jax.numpy as jnp
from jax import lax
from jax.experimental import pallas as pl
from jax.experimental.pallas import tpu as pltpu
from jax.sharding import PartitionSpec as P

F32 = jnp.float32
BF16 = jnp.bfloat16
MESH = pl.DeviceIdType.MESH
CHUNK = 4
NFIELD = 10
R0, W0, Q0, R1, W1, Q1, D1, S1, R2, W2 = range(NFIELD)


def facing_offsets(dev_count):
    return (1, -1, dev_count // 16, -(dev_count // 16), dev_count // 4, -(dev_count // 4))


def split(x):
    hi = x.astype(BF16)
    lo = (x - hi.astype(F32)).astype(BF16)
    return hi, lo


def nn(a, b):
    return lax.dot_general(a, b, (((1,), (0,)), ((), ())), preferred_element_type=F32)


def nt(a, b):
    return lax.dot_general(a, b, (((1,), (1,)), ((), ())), preferred_element_type=F32)


def kernel(n, link_rows, rhs_hbm, band_hbm, link_hbm, sol, res,
           rhs, band, link, wt, lk, hl, wf, wband, hsend, hrecv0, hrecv1, hrecv2, gsend, gall, inv,
           load_sem, hs_sem, hr_sem, gs_sem, gr_sem):
    rows, s, bs = rhs.shape
    faces, slots = link.shape[:2]
    chunks = rows // CHUNK
    me = lax.axis_index("dom")
    offsets = facing_offsets(n)
    nslots = faces * slots
    hrecv = (hrecv0, hrecv1, hrecv2)

    rhs_copy = pltpu.make_async_copy(rhs_hbm, rhs, load_sem.at[0])
    link_copy = pltpu.make_async_copy(link_hbm.at[0], link, load_sem.at[1])

    def band_copy(c):
        at = pl.ds(c * CHUNK, CHUNK)
        return pltpu.make_async_copy(band_hbm.at[at], band.at[at], load_sem.at[2 + c])

    rhs_copy.start()
    link_copy.start()
    for c in range(chunks):
        band_copy(c).start()

    barrier = pltpu.get_barrier_semaphore()

    @pl.loop(1, n)
    def _(k):
        pl.semaphore_signal(barrier, inc=1, device_id=(lax.rem(me + k, n),), device_id_type=MESH)

    @pl.loop(0, rows)
    def _(r):
        for j in range(faces):
            found = jnp.int32(nslots)
            for t in range(slots):
                found = jnp.where(link_rows[0, j, t] == r, jnp.int32(j * slots + t), found)
            inv[r * faces + j] = found

    zero_pad = jnp.zeros((2 * s, bs), BF16)
    for f in (R0, W0, W1):
        for r in (0, 1, rows + 2, rows + 3):
            hl[f, r] = zero_pad
    zero_block = jnp.zeros((bs, 2 * bs), BF16)
    for r, m in ((2, 0), (2, 1), (3, 0), (rows, 4), (rows + 1, 3), (rows + 1, 4)):
        wt[r, m * bs:(m + 1) * bs, :] = zero_block
    for p in range(3):
        hrecv[p][nslots] = jnp.zeros((s, bs), F32)

    def put(f, r, x):
        hi, lo = split(x)
        hl[f, r + 2] = jnp.concatenate([hi, lo], axis=0)

    rhs_copy.wait()

    @pl.loop(0, rows // 4)
    def _(q):
        for u in range(4):
            r = q * 4 + u
            put(R0, r, rhs[r])

    link_copy.wait()

    @pl.loop(0, faces)
    def _(j):
        for t in range(slots):
            hi, lo = split(link[j, t])
            lk[j * slots + t] = jnp.concatenate([hi, lo], axis=1)

    def fold(x):
        half = x.shape[1] // 2
        y = x[:, :half] + x[:, half:]
        return y[:s] + y[s:]

    def halo(p, j):
        peer = lax.rem(me + offsets[j] + n, n)
        return pltpu.make_async_remote_copy(
            src_ref=hsend.at[p, pl.ds(j * slots, slots)],
            dst_ref=hrecv[p].at[pl.ds((j ^ 1) * slots, slots)],
            send_sem=hs_sem.at[p, j], recv_sem=hr_sem.at[p, j ^ 1],
            device_id=(peer,), device_id_type=MESH)

    def halo_arrived(p, j):
        return pltpu.make_async_remote_copy(
            src_ref=hsend.at[p, pl.ds(j * slots, slots)],
            dst_ref=hrecv[p].at[pl.ds(j * slots, slots)],
            send_sem=hs_sem.at[p, j], recv_sem=hr_sem.at[p, j],
            device_id=(me,), device_id_type=MESH)

    def halo_products(p, f):
        for j in range(faces):
            for t in range(slots):
                v = hl[f, link_rows[0, j, t] + 2]
                hsend[p, j * slots + t] = fold(nn(v, lk[j * slots + t]))

    def halo_start(p):
        for j in (4, 5, 2, 3, 0, 1):
            halo(p, j).start()

    def band_rows(f, first):
        for u in range(CHUNK):
            r = first + u
            v = jnp.concatenate([hl[f, r + m] for m in range(5)], axis=1)
            wband[r] = fold(nn(v, wt[r + 2]))

    def collect(p, f, keep):
        for j in range(faces):
            halo_arrived(p, j).wait_recv()

        @pl.loop(0, rows // 4)
        def _(q):
            for u in range(4):
                r = q * 4 + u
                w = wband[r]
                for j in range(faces):
                    w = w + hrecv[p][inv[r * faces + j]]
                if keep:
                    wf[r] = w
                put(f, r, w)

    lane = lax.broadcasted_iota(jnp.int32, (s, 128), 1)
    lane8 = lax.broadcasted_iota(jnp.int32, (s // 2, 128), 1)
    sub = lax.broadcasted_iota(jnp.int32, (s, 128), 0)

    def only(x):
        return jnp.where(lane < s, x, 0.0)

    def roll(x, by):
        return pltpu.roll(x, by % 128, 1)

    def gram_start(p, fr, fw, fd):
        def body(q, acc):
            for u in range(4):
                a, b = 4 * q + u + 2, 0
                right = jnp.concatenate(
                    [hl[fr, a], hl[fw, a], hl[fd, a], jnp.zeros((2 * s, bs), BF16)], axis=0)
                acc = acc + nt(right[:4 * s], right)
            return acc
        c = lax.fori_loop(0, rows // 4, body, jnp.zeros((4 * s, 128), F32))
        cr = c[:s] + c[s:2 * s]
        cw = c[2 * s:3 * s] + c[3 * s:]
        tr = cr + roll(cr, -s)
        tw = cw + roll(cw, -s)
        g = jnp.where(lane < s, tr, jnp.where(lane < 2 * s, roll(tw, -3 * s), jnp.where(lane < 3 * s, tr, 0.0)))
        msg = g[:s // 2] + roll(g[s // 2:], 64)
        gsend[p] = msg
        gall[p, me] = msg

        @pl.loop(1, n)
        def _(k):
            gram_copy(p, lax.rem(me + k, n), me, k).start()

    def gram_copy(p, peer, source, k):
        return pltpu.make_async_remote_copy(
            src_ref=gsend.at[p], dst_ref=gall.at[p, source],
            send_sem=gs_sem.at[p, k], recv_sem=gr_sem.at[p, source],
            device_id=(peer,), device_id_type=MESH)

    def gram_sum(p):
        @pl.loop(1, n)
        def _(k):
            source = lax.rem(me + k, n)
            gram_copy(p, source, source, k).wait_recv()
        total = jnp.sum(gall[p], axis=0)
        full = jnp.concatenate([jnp.where(lane8 < 64, total, 0.0),
                                jnp.where(lane8 < 64, roll(total, 64), 0.0)], axis=0)
        return only(full), only(roll(full, -s)), only(roll(full, -2 * s))

    def transpose(x):
        tall = jnp.concatenate([x, jnp.zeros((128 - s, 128), F32)], axis=0)
        return jnp.transpose(tall)[:s]

    def sym(x):
        return 0.5 * (x + transpose(x))

    def mul(a, b):
        return lax.dot_general(a[:, :s], b, (((1,), (0,)), ((), ())),
                               precision=lax.Precision.HIGHEST, preferred_element_type=F32)

    def solve(g, c):
        m = g + roll(c, s)
        for k in range(s):
            row = m[k:k + 1, :]
            scaled = row / row[:, k:k + 1]
            m = jnp.where(sub == k, scaled, m - m[:, k:k + 1] * scaled)
        return only(roll(m, -s))

    def mixer(blocks, outs):
        tall = [b for b in blocks for _ in range(2)]
        tall = tall + [jnp.zeros((128 - s * len(tall), 128), F32)]
        t = jnp.transpose(jnp.concatenate(tall, axis=0))[:outs * s, :2 * s * len(blocks)]
        hi, lo = split(t)
        return jnp.concatenate([hi, lo], axis=0)

    def mix(m, fields, r):
        u = jnp.concatenate([hl[f, r + 2] for f in fields], axis=0)
        y = nn(m, u)
        half = y.shape[0] // 2
        return y[:half] + y[half:]

    halo_products(0, R0)
    pl.semaphore_wait(barrier, n - 1)
    halo_start(0)

    def convert(c):
        band_copy(c).wait()

        @pl.loop(0, CHUNK)
        def _(u):
            h = c * CHUNK + u
            for b in range(5):
                hi, lo = split(band[h, b])
                wt[h + b, (4 - b) * bs:(5 - b) * bs, :bs] = hi
                wt[h + b, (4 - b) * bs:(5 - b) * bs, bs:] = lo

    convert(0)

    @pl.loop(1, chunks)
    def _(c):
        convert(c)
        band_rows(R0, (c - 1) * CHUNK)

    band_rows(R0, rows - CHUNK)
    collect(0, W0, True)
    gram_start(0, R0, W0, R0)

    def apply(p, fin, fout):
        halo_products(p, fin)
        halo_start(p)

        @pl.loop(0, rows // CHUNK)
        def _(q):
            band_rows(fin, q * CHUNK)
        collect(p, fout, False)

    apply(1, W0, Q0)
    rr, _, rw = gram_sum(0)
    rr0 = sym(rr)
    k0 = sym(rw)
    alpha = solve(k0, rr0)
    m0 = mixer([alpha], 1)

    @pl.loop(0, rows // 2)
    def _(q):
        for u in range(2):
            r = q * 2 + u
            sol[r] = mix(m0, [R0], r)
            x = rhs[r] - mix(m0, [W0], r)
            res[r] = x
            put(R1, r, x)
            w = wf[r] - mix(m0, [Q0], r)
            wf[r] = w
            put(W1, r, w)

    gram_start(1, R1, W1, R0)
    eye = jnp.where(sub == lane, 1.0, 0.0).astype(F32)
    inv0 = solve(rr0, eye)
    apply(2, W1, Q1)

    def coefficients(p, inverse, curv):
        rr, wd, rw = gram_sum(p)
        fresh = sym(rr)
        beta = mul(inverse, fresh)
        beta_t = mul(fresh, inverse)
        curv = sym(rw + mul(2.0 * wd + mul(beta_t, curv), beta))
        alpha = solve(curv, fresh)
        return fresh, curv, beta, alpha, mul(beta, alpha)

    rr1, k1, beta, alpha, gamma = coefficients(1, inv0, k0)
    m1 = mixer([beta + roll(gamma, s), roll(alpha, s)], 2)

    @pl.loop(0, rows // 2)
    def _(q):
        for u in range(2):
            r = q * 2 + u
            y = mix(m1, [R0, R1], r)
            put(D1, r, res[r] + y[:s])
            sol[r] = sol[r] + y[s:]
            y = mix(m1, [W0, W1], r)
            put(S1, r, wf[r] + y[:s])
            x = res[r] - y[s:]
            res[r] = x
            put(R2, r, x)
            y = mix(m1, [Q0, Q1], r)
            put(W2, r, wf[r] - y[s:])

    gram_start(2, R2, W2, D1)
    inv1 = solve(rr1, eye)
    _, _, _, alpha, gamma = coefficients(2, inv1, k1)
    m2 = mixer([alpha, gamma], 1)

    @pl.loop(0, rows // 2)
    def _(q):
        for u in range(2):
            r = q * 2 + u
            sol[r] = sol[r] + mix(m2, [R2, D1], r)
            res[r] = res[r] - mix(m2, [W2, S1], r)

    for p in range(3):
        for j in range(faces):
            halo(p, j).wait_send()

        @pl.loop(1, n)
        def _(k):
            gram_copy(p, lax.rem(me + k, n), me, k).wait_send()


def shards(right_side, band_blocks, link_blocks, link_rows):
    n = lax.axis_size("dom")
    rows, s, bs = right_side.shape
    faces, slots = link_blocks.shape[1:3]
    field = jax.ShapeDtypeStruct(right_side.shape, F32)
    any_spec = pl.BlockSpec(memory_space=pl.ANY)
    vmem = pl.BlockSpec(memory_space=pltpu.VMEM)
    return pl.pallas_call(
        functools.partial(kernel, n),
        out_shape=(field, field),
        in_specs=[pl.BlockSpec(memory_space=pltpu.SMEM), any_spec, any_spec, any_spec],
        out_specs=(vmem, vmem),
        scratch_shapes=[
            pltpu.VMEM((rows, s, bs), F32),
            pltpu.VMEM((rows, 5, bs, bs), F32),
            pltpu.VMEM((faces, slots, bs, bs), F32),
            pltpu.VMEM((rows + 4, 5 * bs, 2 * bs), BF16),
            pltpu.VMEM((faces * slots, bs, 2 * bs), BF16),
            pltpu.VMEM((NFIELD, rows + 4, 2 * s, bs), BF16),
            pltpu.VMEM((rows, s, bs), F32),
            pltpu.VMEM((rows, s, bs), F32),
            pltpu.VMEM((3, faces * slots, s, bs), F32),
            pltpu.VMEM((faces * slots + 1, s, bs), F32),
            pltpu.VMEM((faces * slots + 1, s, bs), F32),
            pltpu.VMEM((faces * slots + 1, s, bs), F32),
            pltpu.VMEM((3, s // 2, 128), F32),
            pltpu.VMEM((3, n, s // 2, 128), F32),
            pltpu.SMEM((rows * faces,), jnp.int32),
            pltpu.SemaphoreType.DMA((2 + rows // CHUNK,)),
            pltpu.SemaphoreType.DMA((3, faces)),
            pltpu.SemaphoreType.DMA((3, faces)),
            pltpu.SemaphoreType.DMA((3, n)),
            pltpu.SemaphoreType.DMA((3, n)),
        ],
        compiler_params=pltpu.CompilerParams(
            collective_id=0, has_side_effects=True, vmem_limit_bytes=60 * 1024 * 1024),
    )(link_rows, right_side, band_blocks, link_blocks)


def solution(mesh):
    in_specs = (
        P("dom", None, None),
        P("dom", None, None, None),
        P("dom", None, None, None, None),
        P("dom", None, None),
    )
    out_specs = (P("dom", None, None), P("dom", None, None))
    return jax.shard_map(shards, mesh=mesh, in_specs=in_specs, out_specs=out_specs, check_vma=False)
```

profile of v0, /device:TPU:0, one launch (start us, length us, event | category | flops | bytes accessed | tf_op | source)
XLA Modules:
  0.0 62.6 jit_solution(2709029625185374798)
XLA Ops:
  0.6 1.4 %copy.6.link_rows = s32[1,6,4]{2,1,0:T(8,128)} copy(s32[1,6,4]{1,2,0:T(4,128)} %param.7) | data formatting | bytes 192 | tf_op args[3]
  2.0 57.2 %shard_map.59 = (f32[32,16,128]{2,1,0:T(8,128)}, f32[32,16,128]{2,1,0:T(8,128)}) custom-call(s32[1,6,4]{2,1,0:T(8,128)} %copy.6.link_rows, f32[32,16,128]{2,1,0:T(8,128)} %rhs_hbm.1, f32[32,5,128,128]{3,2,1,0:T(8,128)} %band_hbm.1, f32[1,6,4,128,128]{4,3,2,1,0:T(8,128)} %link_hbm.1), custom_call_target="tpu_custom_call" | custom-call | tf_op jit(solution)/shard_map/pallas_call | solution.py:348
  59.2 1.7 %copy.9 = f32[32,16,128]{2,1,0:T(8,128)} copy(f32[32,16,128]{2,1,0:T(8,128)} %get-tuple-element.4) | data formatting | bytes 524288
  60.9 1.7 %copy.10 = f32[32,16,128]{2,1,0:T(8,128)} copy(f32[32,16,128]{2,1,0:T(8,128)} %get-tuple-element.5) | data formatting | bytes 524288
where the time goes:
time: 62.8 us; the launch traced here: 62.6 us
  Pallas kernels  57.2 us (91%)
  local copies, waits for them, and re-layouts  4.69 us (7%)
  between operations  0.64 us (1%)
    pallas_call x1, Pallas kernels, shards(): pl.pallas_call(functools.partial(kernel, n), out_shape=(field, field), in...  57.2 us
    unnamed x3, local copies, waits for them, and re-layouts  4.69 us

commit v1 on v0

--- a/solution.py
+++ b/solution.py
@@ -67,7 +67,7 @@
         for j in range(faces):
             found = jnp.int32(nslots)
             for t in range(slots):
-                found = jnp.where(link_rows[0, j, t] == r, jnp.int32(j * slots + t), found)
+                found = jnp.where(link_rows[0, t, j] == r, jnp.int32(j * slots + t), found)
             inv[r * faces + j] = found
 
     zero_pad = jnp.zeros((2 * s, bs), BF16)
@@ -123,7 +123,7 @@
     def halo_products(p, f):
         for j in range(faces):
             for t in range(slots):
-                v = hl[f, link_rows[0, j, t] + 2]
+                v = hl[f, link_rows[0, t, j] + 2]
                 hsend[p, j * slots + t] = fold(nn(v, lk[j * slots + t]))
 
     def halo_start(p):
@@ -131,10 +131,17 @@
             halo(p, j).start()
 
     def band_rows(f, first):
-        for u in range(CHUNK):
+        none = jnp.zeros((2 * s, bs), BF16)
+        deep = 4 * bs
+        for u in range(0, CHUNK, 2):
             r = first + u
-            v = jnp.concatenate([hl[f, r + m] for m in range(5)], axis=1)
-            wband[r] = fold(nn(v, wt[r + 2]))
+            v = [hl[f, r + m] for m in range(6)]
+            pair = jnp.concatenate([jnp.concatenate([v[4], none], axis=1),
+                                    jnp.concatenate([none, v[5]], axis=1)], axis=0)
+            last = nn(pair, jnp.concatenate([wt[r + 2, deep:], wt[r + 3, deep:]], axis=0))
+            for i in range(2):
+                y = nn(jnp.concatenate(v[i:i + 4], axis=1), wt[r + 2 + i, :deep])
+                wband[r + i] = fold(y + last[2 * s * i:2 * s * (i + 1)])
 
     def collect(p, f, keep):
         for j in range(faces):
@@ -163,10 +170,11 @@
 
     def gram_start(p, fr, fw, fd):
         def body(q, acc):
-            for u in range(4):
-                a, b = 4 * q + u + 2, 0
+            for u in range(2):
+                a = 4 * q + 2 * u + 2
                 right = jnp.concatenate(
-                    [hl[fr, a], hl[fw, a], hl[fd, a], jnp.zeros((2 * s, bs), BF16)], axis=0)
+                    [jnp.concatenate([hl[f, a], hl[f, a + 1]], axis=1) for f in (fr, fw, fd)]
+                    + [jnp.zeros((2 * s, 2 * bs), BF16)], axis=0)
                 acc = acc + nt(right[:4 * s], right)
             return acc
         c = lax.fori_loop(0, rows // 4, body, jnp.zeros((4 * s, 128), F32))
@@ -220,16 +228,24 @@
 
     def mixer(blocks, outs):
         tall = [b for b in blocks for _ in range(2)]
-        tall = tall + [jnp.zeros((128 - s * len(tall), 128), F32)]
-        t = jnp.transpose(jnp.concatenate(tall, axis=0))[:outs * s, :2 * s * len(blocks)]
+        depth = s * len(tall)
+        tall = tall + [jnp.zeros((128 - depth, 128), F32)]
+        t = jnp.transpose(jnp.concatenate(tall, axis=0))[:outs * s]
+        t = jnp.concatenate([roll(t, depth * g) if g else t for g in range(128 // depth)], axis=0)
         hi, lo = split(t)
         return jnp.concatenate([hi, lo], axis=0)
 
     def mix(m, fields, r):
-        u = jnp.concatenate([hl[f, r + 2] for f in fields], axis=0)
+        group = 128 // (2 * s * len(fields))
+        u = jnp.concatenate([
+            jnp.concatenate([hl[f, r + side * group + g + 2] for g in range(group) for f in fields], axis=0)
+            for side in range(2)], axis=1)
         y = nn(m, u)
         half = y.shape[0] // 2
-        return y[:half] + y[half:]
+        y = y[:half] + y[half:]
+        tall = half // group
+        return [y[g * tall:(g + 1) * tall, side * bs:(side + 1) * bs]
+                for side in range(2) for g in range(group)]
 
     halo_products(0, R0)
     pl.semaphore_wait(barrier, n - 1)
@@ -255,17 +271,19 @@
 
     band_rows(R0, rows - CHUNK)
     collect(0, W0, True)
-    gram_start(0, R0, W0, R0)
+
+    def send_products(p, f):
+        halo_products(p, f)
+        halo_start(p)
 
     def apply(p, fin, fout):
-        halo_products(p, fin)
-        halo_start(p)
-
         @pl.loop(0, rows // CHUNK)
         def _(q):
             band_rows(fin, q * CHUNK)
         collect(p, fout, False)
 
+    send_products(1, W0)
+    gram_start(0, R0, W0, R0)
     apply(1, W0, Q0)
     rr, _, rw = gram_sum(0)
     rr0 = sym(rr)
@@ -273,18 +291,20 @@
     alpha = solve(k0, rr0)
     m0 = mixer([alpha], 1)
 
-    @pl.loop(0, rows // 2)
+    @pl.loop(0, rows // 8)
     def _(q):
-        for u in range(2):
-            r = q * 2 + u
-            sol[r] = mix(m0, [R0], r)
-            x = rhs[r] - mix(m0, [W0], r)
+        xs, rs, ws = [mix(m0, [f], q * 8) for f in (R0, W0, Q0)]
+        for u in range(8):
+            r = q * 8 + u
+            sol[r] = xs[u]
+            x = rhs[r] - rs[u]
             res[r] = x
             put(R1, r, x)
-            w = wf[r] - mix(m0, [Q0], r)
+            w = wf[r] - ws[u]
             wf[r] = w
             put(W1, r, w)
 
+    send_products(2, W1)
     gram_start(1, R1, W1, R0)
     eye = jnp.where(sub == lane, 1.0, 0.0).astype(F32)
     inv0 = solve(rr0, eye)
@@ -302,32 +322,33 @@
     rr1, k1, beta, alpha, gamma = coefficients(1, inv0, k0)
     m1 = mixer([beta + roll(gamma, s), roll(alpha, s)], 2)
 
-    @pl.loop(0, rows // 2)
+    @pl.loop(0, rows // 4)
     def _(q):
-        for u in range(2):
-            r = q * 2 + u
-            y = mix(m1, [R0, R1], r)
-            put(D1, r, res[r] + y[:s])
-            sol[r] = sol[r] + y[s:]
-            y = mix(m1, [W0, W1], r)
-            put(S1, r, wf[r] + y[:s])
-            x = res[r] - y[s:]
+        ds, ss, zs = [mix(m1, f, q * 4) for f in ([R0, R1], [W0, W1], [Q0, Q1])]
+        for u in range(4):
+            r = q * 4 + u
+            x = res[r]
+            w = wf[r]
+            put(D1, r, x + ds[u][:s])
+            sol[r] = sol[r] + ds[u][s:]
+            put(S1, r, w + ss[u][:s])
+            x = x - ss[u][s:]
             res[r] = x
             put(R2, r, x)
-            y = mix(m1, [Q0, Q1], r)
-            put(W2, r, wf[r] - y[s:])
+            put(W2, r, w - zs[u][s:])
 
     gram_start(2, R2, W2, D1)
     inv1 = solve(rr1, eye)
     _, _, _, alpha, gamma = coefficients(2, inv1, k1)
     m2 = mixer([alpha, gamma], 1)
 
-    @pl.loop(0, rows // 2)
+    @pl.loop(0, rows // 4)
     def _(q):
-        for u in range(2):
-            r = q * 2 + u
-            sol[r] = sol[r] + mix(m2, [R2, D1], r)
-            res[r] = res[r] - mix(m2, [W2, S1], r)
+        xs, rs = [mix(m2, f, q * 4) for f in ([R2, D1], [W2, S1])]
+        for u in range(4):
+            r = q * 4 + u
+            sol[r] = sol[r] + xs[u]
+            res[r] = res[r] - rs[u]
 
     for p in range(3):
         for j in range(faces):
@@ -336,6 +357,11 @@
         @pl.loop(1, n)
         def _(k):
             gram_copy(p, lax.rem(me + k, n), me, k).wait_send()
+
+
+def hand_over(a, b, c, d):
+    c[...] = a[...]
+    d[...] = b[...]
 
 
 def shards(right_side, band_blocks, link_blocks, link_rows):
@@ -345,7 +371,7 @@
     field = jax.ShapeDtypeStruct(right_side.shape, F32)
     any_spec = pl.BlockSpec(memory_space=pl.ANY)
     vmem = pl.BlockSpec(memory_space=pltpu.VMEM)
-    return pl.pallas_call(
+    pair = pl.pallas_call(
         functools.partial(kernel, n),
         out_shape=(field, field),
         in_specs=[pl.BlockSpec(memory_space=pltpu.SMEM), any_spec, any_spec, any_spec],
@@ -374,7 +400,10 @@
         ],
         compiler_params=pltpu.CompilerParams(
             collective_id=0, has_side_effects=True, vmem_limit_bytes=60 * 1024 * 1024),
-    )(link_rows, right_side, band_blocks, link_blocks)
+    )(jnp.swapaxes(link_rows, 1, 2), right_side, band_blocks, link_blocks)
+
+    return pl.pallas_call(
+        hand_over, out_shape=(field, field), in_specs=[vmem, vmem], out_specs=(vmem, vmem))(*pair)
 
 
 def solution(mesh):

time: 62.8 us -> 52.5 us (0.84)
  Pallas kernels: 57.2 us -> 51.7 us
  local copies, waits for them, and re-layouts: 4.69 us -> 0 us
    pallas_call x1, Pallas kernels: 57.2 us -> 49.8 us  [shards(): pl.pallas_call(functools.partial(kernel, n), out_shape=(field, field), in...]
    unnamed x3 -> x0, local copies, waits for them, and re-layouts: 4.69 us -> none
    pallas_call x0 -> x1, Pallas kernels: none -> 1.84 us  [shards(): pl.pallas_call(hand_over, out_shape=(field, field), in_specs=[vmem, vmem]...]
where the time goes in v1:
time: 52.5 us; the launch traced here: 52.3 us
  Pallas kernels  51.7 us (98%)
  between operations  0.64 us (1%)
    pallas_call x1, Pallas kernels, shards(): pl.pallas_call(functools.partial(kernel, n), out_shape=(field, field), in...  49.8 us
    pallas_call x1, Pallas kernels, shards(): pl.pallas_call(hand_over, out_shape=(field, field), in_specs=[vmem, vmem]...  1.84 us

profile of v1, /device:TPU:0, one launch (start us, length us, event | category | flops | bytes accessed | tf_op | source)
XLA Modules:
  0.0 52.3 jit_solution(3053544291941161484)
XLA Ops:
  0.6 49.8 %shard_map.59 = (f32[32,16,128]{2,1,0:T(8,128)}, f32[32,16,128]{2,1,0:T(8,128)}) custom-call(s32[1,4,6]{2,1,0:T(4,128)} %bitcast.1, f32[32,16,128]{2,1,0:T(8,128)} %rhs_hbm.1, f32[32,5,128,128]{3,2,1,0:T(8,128)} %band_hbm.1, f32[1,6,4,128,128]{4,3,2,1,0:T(8,128)} %link_hbm.1), custom_call_target="tpu_custom_call" | custom-call | tf_op jit(solution)/shard_map/pallas_call | solution.py:374
  50.5 1.8 %shard_map.60 = (f32[32,16,128]{2,1,0:T(8,128)}, f32[32,16,128]{2,1,0:T(8,128)}) custom-call(f32[32,16,128]{2,1,0:T(8,128)} %get-tuple-element.4.a, f32[32,16,128]{2,1,0:T(8,128)} %get-tuple-element.5.b), custom_call_target="tpu_custom_call" | custom-call | tf_op jit(solution)/shard_map/pallas_call | solution.py:405
